TPU v7x, 32 devices: a whole 2x2x4 slice. The times are simulated.
32 devices in a mesh: epoch: 4 (over y, x), blend: 8 (over z, core).
Axes of the slice: x: 2, y: 2, z: 4, core: 2. Of those that a mesh axis runs over, the one named last changes fastest.
Arguments:
- visit_flux: bfloat16 [16, 32, 6, 16384], P('epoch', None, None, 'blend'), may hold values from -6 to 6
- visit_precision: bfloat16 [16, 32, 6, 16384], P('epoch', None, None, 'blend'), may hold values from 0.25 to 4
- visit_live: int32 [16, 32], P('epoch'), may hold values 0 or 1
- footprint: int32 [32, 8, 16384], P('blend', None, 'epoch'), may hold values 0 or 1
- source_count: int32 [32], P('blend'), may hold values from 1 to 8
- spectra_init: float32 [32, 8, 6], P('blend'), may hold values from 0.2 to 1.2
- morphology_init: float32 [32, 8, 16384], P('blend', None, 'epoch'), may hold values from 0 to 0.25
Outputs:
- coadd_flux: float32 [32, 6, 16384], P('blend', None, 'epoch')
- spectra: float32 [32, 8, 6], P('blend')
- morphology: float32 [32, 8, 16384], P('blend', None, 'epoch')
All inputs are finite; a program needn't handle non-finite values. No bound on the sum of `visit_live` or of `footprint` on one device may be relied on, other than what follows from the above.
Results may differ from a plain program's by a relative error of at most 0.0003.
Values sent between devices are 32-bit elements; how exact they have to be, the bound alone decides.
A program may use at most 64 MiB of HBM per device.

v0:
```python
import jax
import jax.numpy as jnp
from jax import lax
from jax.sharding import PartitionSpec as P

ITERS = 2


def on_device(
    visit_flux, visit_precision, visit_live, footprint, source_count, spectra_init, morphology_init
):
    weights = visit_precision.astype(jnp.float32) * visit_live.astype(jnp.float32)[:, :, None, None]
    numerator = jnp.sum(weights * visit_flux.astype(jnp.float32), axis=0)
    weight_sum = jnp.sum(weights, axis=0)
    pix_part = morphology_init.shape[2]
    owned = morphology_init.shape[0]
    numerator, weight_sum = (
        lax.psum_scatter(numerator, "epoch", scatter_dimension=2, tiled=True),
        lax.psum_scatter(weight_sum, "epoch", scatter_dimension=2, tiled=True),
    )
    every_blend, band_count, piece = numerator.shape
    numerator = numerator.reshape(every_blend, band_count, 1, piece)
    weight_sum = weight_sum.reshape(every_blend, band_count, 1, piece)
    numerator, weight_sum = (
        lax.all_to_all(numerator, "blend", split_axis=0, concat_axis=2, tiled=True),
        lax.all_to_all(weight_sum, "blend", split_axis=0, concat_axis=2, tiled=True),
    )
    blocks = numerator.shape[2]
    numerator = numerator.reshape(owned, band_count, blocks, 1, piece)
    weight_sum = weight_sum.reshape(owned, band_count, blocks, 1, piece)
    numerator, weight_sum = (
        lax.all_to_all(numerator, "epoch", split_axis=2, concat_axis=3, tiled=True),
        lax.all_to_all(weight_sum, "epoch", split_axis=2, concat_axis=3, tiled=True),
    )
    numerator = numerator.reshape(owned, band_count, pix_part)
    weight_sum = weight_sum.reshape(owned, band_count, pix_part)
    coadd_flux = numerator / (1.0 + weight_sum)
    coverage = weight_sum / (1.0 + weight_sum)
    slots = footprint.shape[1]
    source_live = (jnp.arange(slots, dtype=jnp.int32)[None, :] < source_count[:, None]).astype(
        jnp.float32
    )
    footprint_mask = footprint.astype(jnp.float32) * source_live[:, :, None]
    live_count = source_count.astype(jnp.float32)
    morphology = morphology_init * footprint_mask
    spectra = spectra_init
    highest = lax.Precision.HIGHEST
    for iteration in range(ITERS):
        blend_model = jnp.einsum("bkc,bkp->bcp", spectra, morphology, precision=highest)
        residual = coverage * (coadd_flux - blend_model)
        morph_grad = jnp.einsum("bkc,bcp->bkp", spectra, residual, precision=highest)
        morph_step = 1.0 / (1.0 + live_count[:, None] * jnp.sum(spectra * spectra, axis=2))
        morphology = (
            jnp.maximum(0.0, morphology + morph_grad * morph_step[:, :, None]) * footprint_mask
        )
        blend_model = jnp.einsum("bkc,bkp->bcp", spectra, morphology, precision=highest)
        residual = coverage * (coadd_flux - blend_model)
        spectra_grad = jnp.einsum("bkp,bcp->bkc", morphology, residual, precision=highest)
        morph_norm = jnp.sum(morphology * morphology, axis=2)
        spectra_grad, morph_norm = lax.psum((spectra_grad, morph_norm), "epoch")
        spectra = jnp.maximum(
            0.0, spectra + spectra_grad / (1.0 + live_count[:, None] * morph_norm)[:, :, None]
        )
    return (coadd_flux, spectra, morphology)


def solution(mesh):
    in_specs = (
        P("epoch", None, None, "blend"),
        P("epoch", None, None, "blend"),
        P("epoch", None),
        P("blend", None, "epoch"),
        P("blend"),
        P("blend", None, None),
        P("blend", None, "epoch"),
    )
    out_specs = (P("blend", None, "epoch"), P("blend", None, None), P("blend", None, "epoch"))
    return jax.shard_map(
        on_device, mesh=mesh, in_specs=in_specs, out_specs=out_specs, check_vma=False
    )
```

profile of v0, /device:TPU:0, one launch (start us, length us, event | category | flops | bytes accessed | tf_op | source)
XLA Modules:
  0.0 167.4 jit_solution(2619093483653560001)
XLA Ops:
  7.2 0.0 reduce-scatter.5.cloned.1.call-start
  7.2 0.7 convert_element_type.23
  7.9 6.4 %fusion = (f32[32,6,2048]{2,0,1:T(8,128)}, f32[32,6,2048]{2,0,1:T(8,128)}) fusion(bf16[4,32,6,2048]{3,1,2,0:T(8,128)(2,1)} %param.8, f32[4,32]{1,0:T(4,128)S(1)} %convert_element_type.23, bf16[4,32,6,2048]{3,1,2,0:T(8,128)(2,1)} %param.7), kind=kLoop, calls=%fused_computation.2 | loop fusion | flops 8650752 | bytes 9437696 | tf_op jit(solution)/shard_map/reduce_sum | solution.py:14
  14.3 0.0 reduce-scatter.5.cloned.1.call-update
  14.3 0.0 reduce-scatter.3.cloned.1.call-start
  14.4 0.0 copy-start.4
  14.4 0.0 copy-start.3
  14.4 0.7 reduce-scatter.3.cloned.1.call-update
  15.1 33.3 %reduce-scatter.5.cloned.1.call-done = f32[32,6,512]{2,0,1:T(8,128)} async-done(((f32[32,6,2048]{2,0,1:T(8,128)}), f32[32,6,512]{2,0,1:T(8,128)}) %reduce-scatter.5.cloned.1.call-update) | async-done | bytes 393232 | tf_op jit(solution)/shard_map/reduce_scatter | solution.py:19
  48.4 2.1 %copy.58 = f32[32,6,1,512]{3,2,1,0:T(1,128)} copy(f32[32,6,1,512]{3,0,1,2:T(8,128)} %bitcast.57) | data formatting | bytes 786432 | tf_op jit(solution)/shard_map/reshape | solution.py:23
  50.5 4.6 %all-to-all-start.2 = ((f32[32,6,1,512]{3,2,1,0:T(1,128)}), f32[32,6,1,512]{3,2,1,0:T(1,128)S(1)}, u32[]{:S(2)}, u32[]{:S(2)}) async-start(f32[32,6,1,512]{3,2,1,0:T(1,128)} %copy.58), calls=%async_computation.4 | async-start | bytes 786432 | tf_op jit(solution)/shard_map/all_to_all | solution.py:26
  55.1 27.4 %reduce-scatter.3.cloned.1.call-done = f32[32,6,512]{2,0,1:T(8,128)} async-done(((f32[32,6,2048]{2,0,1:T(8,128)}), f32[32,6,512]{2,0,1:T(8,128)}) %reduce-scatter.3.cloned.1.call-update) | async-done | bytes 393232 | tf_op jit(solution)/shard_map/reduce_scatter | solution.py:18
  82.5 2.1 %copy.54 = f32[32,6,1,512]{3,2,1,0:T(1,128)} copy(f32[32,6,1,512]{3,0,1,2:T(8,128)} %bitcast.58) | data formatting | bytes 786432 | tf_op jit(solution)/shard_map/reshape | solution.py:22
  84.7 0.0 all-to-all-done.2
  84.7 4.6 %all-to-all-start = ((f32[32,6,1,512]{3,2,1,0:T(1,128)}), f32[32,6,1,512]{3,2,1,0:T(1,128)S(1)}, u32[]{:S(2)}, u32[]{:S(2)}) async-start(f32[32,6,1,512]{3,2,1,0:T(1,128)} %copy.54), calls=%async_computation.1 | async-start | bytes 786432 | tf_op jit(solution)/shard_map/all_to_all | solution.py:25
  89.3 0.8 copy.85
  90.1 11.7 %all-to-all-done = f32[32,6,1,512]{3,2,1,0:T(1,128)S(1)} async-done(((f32[32,6,1,512]{3,2,1,0:T(1,128)}), f32[32,6,1,512]{3,2,1,0:T(1,128)S(1)}, u32[]{:S(2)}, u32[]{:S(2)}) %all-to-all-start) | async-done | bytes 393248 | tf_op jit(solution)/shard_map/all_to_all | solution.py:25
  101.8 3.5 %all-to-all-start.3 = ((f32[4,6,8,1,512]{4,0,1,3,2:T(4,128)}), f32[4,6,8,1,512]{4,0,1,3,2:T(4,128)S(1)}, u32[]{:S(2)}, u32[]{:S(2)}) async-start(f32[4,6,8,1,512]{4,0,1,3,2:T(4,128)} %bitcast.51), calls=%async_computation.5 | async-start | bytes 786432 | tf_op jit(solution)/shard_map/all_to_all | solution.py:33
  105.2 0.0 copy-done.4
  105.3 0.0 copy-done.3
  105.3 0.1 copy.68
  105.4 0.1 fusion.19
  105.4 0.8 copy.86
  106.3 5.2 %all-to-all-done.3 = f32[4,6,8,1,512]{4,0,1,3,2:T(4,128)S(1)} async-done(((f32[4,6,8,1,512]{4,0,1,3,2:T(4,128)}), f32[4,6,8,1,512]{4,0,1,3,2:T(4,128)S(1)}, u32[]{:S(2)}, u32[]{:S(2)}) %all-to-all-start.3) | async-done | bytes 393248 | tf_op jit(solution)/shard_map/all_to_all | solution.py:33
  111.5 3.5 %all-to-all-start.1 = ((f32[4,6,8,1,512]{4,0,1,3,2:T(4,128)}), f32[4,6,8,1,512]{4,0,1,3,2:T(4,128)S(1)}, u32[]{:S(2)}, u32[]{:S(2)}) async-start(f32[4,6,8,1,512]{4,0,1,3,2:T(4,128)} %bitcast.52), calls=%async_computation.2 | async-start | bytes 786432 | tf_op jit(solution)/shard_map/all_to_all | solution.py:32
  115.0 0.1 add_divide_fusion.3
  115.1 0.3 copy.77
  115.4 0.0 copy-start
  115.4 0.0 copy-start.2
  115.4 0.3 reshape.92
  115.7 5.1 %all-to-all-done.1 = f32[4,6,8,1,512]{4,0,1,3,2:T(4,128)S(1)} async-done(((f32[4,6,8,1,512]{4,0,1,3,2:T(4,128)}), f32[4,6,8,1,512]{4,0,1,3,2:T(4,128)S(1)}, u32[]{:S(2)}, u32[]{:S(2)}) %all-to-all-start.1) | async-done | bytes 393248 | tf_op jit(solution)/shard_map/all_to_all | solution.py:32
  120.9 0.3 copy.75
  121.1 0.3 reshape.91
  121.4 0.1 add_divide_fusion.1
  121.5 1.0 copy.71
  122.5 0.0 copy-done
  122.5 0.0 copy-done.2
  122.5 0.7 fusion.13
  123.2 0.8 multiply_reduce_fusion.2
  124.0 0.6 fusion.11
  124.6 1.2 fusion.20
  125.7 15.3 %all-reduce.1 = (f32[4,8,6]{2,1,0:T(8,128)S(1)}, f32[4,8]{1,0:T(4,128)S(1)}) all-reduce(f32[4,8,6]{2,1,0:T(8,128)S(1)} %fusion.20, f32[4,8]{1,0:T(4,128)S(1)} %get-tuple-element.26), channel_id=1, replica_groups=mesh['epoch'=4,'blend'=8] {'epoch'}, use_global_device_ids=true, to_apply=%region_5.0 | all-reduce | flops 224 | bytes 1792 | tf_op jit(solution)/shard_map/psum | solution.py:60
  141.1 0.1 multiply_add_fusion.1
  141.2 0.2 multiply_reduce_fusion.3
  141.3 0.7 fusion.3
  142.0 0.1 add_divide_fusion.2
  142.1 0.8 multiply_reduce_fusion.1
  142.8 0.0 copy-start.1
  142.8 0.7 fusion.1
  143.5 1.2 fusion.21
  144.7 15.1 %all-reduce = (f32[4,8,6]{2,1,0:T(8,128)S(1)}, f32[4,8]{1,0:T(4,128)S(1)}) all-reduce(f32[4,8,6]{2,1,0:T(8,128)S(1)} %fusion.21, f32[4,8]{1,0:T(4,128)S(1)} %get-tuple-element.28), channel_id=1, replica_groups=mesh['epoch'=4,'blend'=8] {'epoch'}, use_global_device_ids=true, to_apply=%region_9.0 | all-reduce | flops 224 | bytes 1792 | tf_op jit(solution)/shard_map/psum | solution.py:60
  159.7 0.1 multiply_add_fusion
  159.8 0.1 add_maximum_fusion
  159.9 0.7 copy.72
  160.6 0.0 copy-done.1
  (4 shorter events, 0.1 us)
Async XLA Ops:
  7.2 41.2 %reduce-scatter.5.cloned.1.call-start = ((), (), s32[]{:S(2)}) async-start(), calls=%async_computation.7 | async-start | bytes 1966080 | tf_op jit(solution)/shard_map/reduce_scatter | solution.py:19
  14.3 68.2 %reduce-scatter.3.cloned.1.call-start = ((), (), s32[]{:S(2)}) async-start(), calls=%async_computation.6 | async-start | bytes 1966080 | tf_op jit(solution)/shard_map/reduce_scatter | solution.py:18
  14.4 90.9 %copy-start.4 = (s32[4]{0:T(128)S(1)}, s32[4]{0:T(128)}, u32[]{:S(2)}) copy-start(s32[4]{0:T(128)} %param.11) | copy-start | bytes 52
  14.4 90.9 %copy-start.3 = (f32[4,8,6]{1,0,2:T(4,128)S(1)}, f32[4,8,6]{1,0,2:T(4,128)}, u32[]{:S(2)}) copy-start(f32[4,8,6]{1,0,2:T(4,128)} %param.12) | copy-start | bytes 2308
  50.5 34.1 %all-to-all-start.2 = ((f32[32,6,1,512]{3,2,1,0:T(1,128)}), f32[32,6,1,512]{3,2,1,0:T(1,128)S(1)}, u32[]{:S(2)}, u32[]{:S(2)}) async-start(f32[32,6,1,512]{3,2,1,0:T(1,128)} %copy.58), calls=%async_computation.4 | async-start | bytes 786432 | tf_op jit(solution)/shard_map/all_to_all | solution.py:26
  84.7 17.1 %all-to-all-start = ((f32[32,6,1,512]{3,2,1,0:T(1,128)}), f32[32,6,1,512]{3,2,1,0:T(1,128)S(1)}, u32[]{:S(2)}, u32[]{:S(2)}) async-start(f32[32,6,1,512]{3,2,1,0:T(1,128)} %copy.54), calls=%async_computation.1 | async-start | bytes 786432 | tf_op jit(solution)/shard_map/all_to_all | solution.py:25
  101.8 9.7 %all-to-all-start.3 = ((f32[4,6,8,1,512]{4,0,1,3,2:T(4,128)}), f32[4,6,8,1,512]{4,0,1,3,2:T(4,128)S(1)}, u32[]{:S(2)}, u32[]{:S(2)}) async-start(f32[4,6,8,1,512]{4,0,1,3,2:T(4,128)} %bitcast.51), calls=%async_computation.5 | async-start | bytes 786432 | tf_op jit(solution)/shard_map/all_to_all | solution.py:33
  111.5 9.3 %all-to-all-start.1 = ((f32[4,6,8,1,512]{4,0,1,3,2:T(4,128)}), f32[4,6,8,1,512]{4,0,1,3,2:T(4,128)S(1)}, u32[]{:S(2)}, u32[]{:S(2)}) async-start(f32[4,6,8,1,512]{4,0,1,3,2:T(4,128)} %bitcast.52), calls=%async_computation.2 | async-start | bytes 786432 | tf_op jit(solution)/shard_map/all_to_all | solution.py:32
  115.4 7.1 %copy-start = (s32[4,8,4096]{2,1,0:T(8,128)S(1)}, s32[4,8,4096]{2,1,0:T(8,128)}, u32[]{:S(2)}) copy-start(s32[4,8,4096]{2,1,0:T(8,128)} %param.10) | copy-start | bytes 1572868
  115.4 7.1 %copy-start.2 = (f32[4,8,4096]{2,1,0:T(8,128)S(1)}, f32[4,8,4096]{2,1,0:T(8,128)}, u32[]{:S(2)}) copy-start(f32[4,8,4096]{2,1,0:T(8,128)} %param.13) | copy-start | bytes 1572868
  142.8 17.7 %copy-start.1 = (f32[4,8,4096]{2,1,0:T(8,128)}, f32[4,8,4096]{2,1,0:T(8,128)S(1)}, u32[]{:S(2)}) copy-start(f32[4,8,4096]{2,1,0:T(8,128)S(1)} %get-tuple-element.29) | copy-start | bytes 1572868
Sparse Core Ops, SparseCore 0:
  14.5 33.8 reduce-scatter.4
  51.4 31.1 reduce-scatter.2
where the time goes:
time: 168 us; the launch traced here: 167 us
  waiting for transfers between devices  83.4 us (50%)
  blocking collectives  30.4 us (18%)
  starting transfers between devices  16.2 us (10%)
  between operations  14.2 us (8%)
  local copies, waits for them, and re-layouts  8.92 us (5%)
  other arithmetic  7.82 us (5%)
  matrix products  6.48 us (4%)
    reduce_scatter x1, waiting for transfers between devices, on_device(): lax.psum_scatter(weight_sum, 'epoch', scatter_dimension=2, tiled=True)  33.3 us
    psum x2, blocking collectives, on_device(): spectra_grad, morph_norm = lax.psum((spectra_grad, morph_norm), 'epoch')  30.4 us
    reduce_scatter x1, waiting for transfers between devices, on_device(): lax.psum_scatter(numerator, 'epoch', scatter_dimension=2, tiled=True)  27.4 us
    all_to_all x1, waiting for transfers between devices, on_device(): lax.all_to_all(numerator, 'blend', split_axis=0, concat_axis=2, tiled=True)  11.7 us
    reduce_sum x1, other arithmetic, on_device(): weight_sum = jnp.sum(weights, axis=0)  6.42 us
    all_to_all x1, waiting for transfers between devices, on_device(): lax.all_to_all(weight_sum, 'epoch', split_axis=2, concat_axis=3, tiled=True)  5.22 us
    all_to_all x1, waiting for transfers between devices, on_device(): lax.all_to_all(numerator, 'epoch', split_axis=2, concat_axis=3, tiled=True)  5.14 us
    all_to_all x1, starting transfers between devices, on_device(): lax.all_to_all(weight_sum, 'blend', split_axis=0, concat_axis=2, tiled=True)  4.59 us
  transfers between devices with their start and end apart: 6, of which 5 were waited for; matrix products, arithmetic and copies ran while one was open for 4% of the time, Pallas kernels for 0%

commit v1 on v0

--- a/solution.py
+++ b/solution.py
@@ -1,9 +1,424 @@
+import functools
+
 import jax
 import jax.numpy as jnp
 from jax import lax
+from jax.experimental import pallas as pl
+from jax.experimental.pallas import tpu as pltpu
 from jax.sharding import PartitionSpec as P
 
 ITERS = 2
+
+
+LANES = 128
+MESH = pl.DeviceIdType.MESH
+
+
+def factors(count):
+    rows = max(d for d in range(1, count + 1) if count % d == 0 and d * d <= count)
+    return rows, count // rows
+
+
+def coadd_kernel(
+    flux_hbm, prec_hbm, live_ref, foot_hbm, count_ref, spec_ref, morph_hbm,
+    coadd_ref, spec_out, morph_ref,
+    flux_v, prec_v, foot_v, cover,
+    stage, land1, part, land2, final, pieces, by_band, by_source, step_ref, acc, sums,
+    in_sem, side_sem, s1_send, s1_recv, s2_send, s2_recv, s3_send, s3_recv, ps_send, ps_recv,
+    *, ne, nb, ny, nx,
+):
+    visits, every_blend, bands, block = flux_hbm.shape
+    owned, slots, pix_part = morph_hbm.shape
+    chunks = flux_v.shape[0]
+    width = block // chunks
+    per_dest = pix_part // block
+    e = lax.axis_index("epoch")
+    j = lax.axis_index("blend")
+    y, x = e // nx, e % nx
+    home_e = j // per_dest
+    home_slot = j % per_dest
+    f32 = jnp.float32
+
+    def in_copy(q):
+        window = pl.ds(q * width, width)
+        return (
+            pltpu.make_async_copy(flux_hbm.at[:, :, :, window], flux_v.at[q], in_sem.at[0, q]),
+            pltpu.make_async_copy(prec_hbm.at[:, :, :, window], prec_v.at[q], in_sem.at[1, q]),
+        )
+
+    for q in range(chunks):
+        for copy in in_copy(q):
+            copy.start()
+    side = (
+        pltpu.make_async_copy(foot_hbm, foot_v, side_sem.at[0]),
+        pltpu.make_async_copy(morph_hbm, morph_ref, side_sem.at[1]),
+    )
+    for copy in side:
+        copy.start()
+
+    barrier = pltpu.get_barrier_semaphore()
+    total = ne * nb
+    mine = e * nb + j
+
+    def greet(d, carry):
+        other = lax.rem(mine + d, total)
+        pl.semaphore_signal(
+            barrier, inc=1, device_id=(other // nb, lax.rem(other, nb)), device_id_type=MESH
+        )
+        return carry
+
+    lax.fori_loop(1, total, greet, 0)
+
+    def local_sum(q):
+        for copy in in_copy(q):
+            copy.wait()
+
+        def one(dest, carry):
+            for b in range(owned):
+                blend = dest * owned + b
+                num = None
+                for v in range(visits):
+                    w = prec_v[q, v, blend].astype(f32) * live_ref[v, blend].astype(f32)
+                    n = w * flux_v[q, v, blend].astype(f32)
+                    num, wsum = (n, w) if num is None else (num + n, wsum + w)
+                for p in range(ne):
+                    py, px = p // nx, p % nx
+                    lanes = slice(p * LANES, (p + 1) * LANES)
+                    rows = slice(b * bands, (b + 1) * bands)
+                    stage[0, q, px * ny + py, dest, rows, :] = num[:, lanes]
+                    stage[1, q, py * nx + px, dest, rows, :] = wsum[:, lanes]
+            return carry
+
+        lax.fori_loop(0, nb, one, 0)
+
+    def line(a, first):
+        along_x = (a == 0) == first
+        return (x, nx) if along_x else (y, ny)
+
+    def device_at(a, first, where):
+        along_x = (a == 0) == first
+        return (y * nx + where if along_x else where * nx + x, j)
+
+    def s1(a, q, d):
+        at, n = line(a, True)
+        other = line(a, False)[1]
+        to = lax.rem(at + d, n)
+        return pltpu.make_async_remote_copy(
+            src_ref=stage.at[a, q, pl.ds(to * other, other)],
+            dst_ref=land1.at[a, q, d - 1],
+            send_sem=s1_send.at[a, q, d - 1], recv_sem=s1_recv.at[a, q, d - 1],
+            device_id=device_at(a, True, to), device_id_type=MESH,
+        )
+
+    def s2(a, q, d):
+        at, n = line(a, False)
+        to = lax.rem(at + d, n)
+        return pltpu.make_async_remote_copy(
+            src_ref=part.at[a, q, to],
+            dst_ref=land2.at[a, q, d - 1],
+            send_sem=s2_send.at[a, q, d - 1], recv_sem=s2_recv.at[a, q, d - 1],
+            device_id=device_at(a, False, to), device_id_type=MESH,
+        )
+
+    def s1_start(q):
+        for a in range(2):
+            for d in range(1, line(a, True)[1]):
+                s1(a, q, d).start()
+
+    def s2_start(q):
+        for a in range(2):
+            at, n = line(a, True)
+            others = line(a, False)[1]
+            for d in range(1, n):
+                s1(a, q, d).wait_recv()
+
+            def add(i, carry):
+                o, dest = i // nb, lax.rem(i, nb)
+                v = stage[a, q, at * others + o, dest]
+                for d in range(1, n):
+                    v = v + land1[a, q, d - 1, o, dest]
+                part[a, q, o, dest] = v
+                return carry
+
+            lax.fori_loop(0, others * nb, add, 0)
+            for d in range(1, others):
+                s2(a, q, d).start()
+
+    here = home_e == e
+
+    def s3_local(q):
+        return pltpu.make_async_copy(
+            final.at[q, j],
+            pieces.at[q, :, :, pl.ds(pl.multiple_of(home_slot * width + e * LANES, LANES), LANES)],
+            s3_recv.at[q],
+        )
+
+    def s3_remote(q, to):
+        return pltpu.make_async_remote_copy(
+            src_ref=final.at[q, to],
+            dst_ref=pieces.at[
+                q, :, :, pl.ds(pl.multiple_of(home_slot * width + e * LANES, LANES), LANES)
+            ],
+            send_sem=s3_send.at[q, to], recv_sem=s3_recv.at[q],
+            device_id=(home_e, to), device_id_type=MESH,
+        )
+
+    def s3_start(q):
+        for a in range(2):
+            at, n = line(a, False)
+            for d in range(1, n):
+                s2(a, q, d).wait_recv()
+
+            def add(dest, carry):
+                v = part[a, q, at, dest]
+                for d in range(1, n):
+                    v = v + land2[a, q, d - 1, dest]
+                final[q, dest, a] = v
+                return carry
+
+            lax.fori_loop(0, nb, add, 0)
+
+        def send(d, carry):
+            to = lax.rem(j + d, nb)
+            s3_remote(q, to).start()
+            return carry
+
+        lax.fori_loop(1, nb, send, 0)
+
+        @pl.when(here)
+        def _():
+            s3_local(q).start()
+
+        @pl.when(jnp.logical_not(here))
+        def _():
+            s3_remote(q, j).start()
+
+    sub = lax.broadcasted_iota(jnp.int32, (slots, LANES), 0)
+    lane = lax.broadcasted_iota(jnp.int32, (slots, LANES), 1)
+
+    def spread():
+        for b in range(owned):
+            norm = None
+            for c in range(bands):
+                s = by_band[b, c]
+                norm = s * s if norm is None else norm + s * s
+            step_ref[b] = 1.0 / (1.0 + count_ref[b].astype(f32) * norm)
+
+        def move(b, carry):
+            for k in range(slots):
+                for c in range(bands):
+                    by_source[b, k, c : c + 1, :] = by_band[b, c, k : k + 1, :]
+            return carry
+
+        lax.fori_loop(0, owned, move, 0)
+
+    def deblend(b, start, first):
+        live = jnp.where(sub < count_ref[b], 1.0, 0.0).astype(f32)
+        step = step_ref[b]
+        bs = [by_source[b, k] for k in range(slots)]
+        bb = [by_band[b, c] for c in range(bands)]
+        grads = [acc[b, c] for c in range(bands + 1)]
+
+        for t in range(width // LANES):
+            px = pl.ds(pl.multiple_of(start + t * LANES, LANES), LANES)
+            mask = foot_v[b, :, px].astype(f32) * live
+            morph = morph_ref[b, :, px]
+            if first:
+                morph = morph * mask
+            cov = cover[b, :, px]
+            flux = coadd_ref[b, :, px]
+
+            def residual(m):
+                model = bs[0] * m[0:1, :]
+                for k in range(1, slots):
+                    model = model + bs[k] * m[k : k + 1, :]
+                return cov * (flux - model)
+
+            res = residual(morph)
+            grad = bb[0] * res[0:1, :]
+            for c in range(1, bands):
+                grad = grad + bb[c] * res[c : c + 1, :]
+            morph = jnp.maximum(0.0, morph + grad * step) * mask
+            morph_ref[b, :, px] = morph
+            res = residual(morph)
+            for c in range(bands):
+                grads[c] = grads[c] + morph * res[c : c + 1, :]
+            grads[bands] = grads[bands] + morph * morph
+        for c in range(bands + 1):
+            acc[b, c] = grads[c]
+
+    def finish(q):
+        pltpu.make_async_copy(pieces.at[q], pieces.at[q], s3_recv.at[q]).wait()
+        for s in range(per_dest):
+            src = slice(s * width, (s + 1) * width)
+            dst = slice(s * block + q * width, s * block + (q + 1) * width)
+            for b in range(owned):
+                rows = slice(b * bands, (b + 1) * bands)
+                wsum = pieces[q, 1, rows, src]
+                inv = 1.0 / (1.0 + wsum)
+                coadd_ref[b, :, dst] = pieces[q, 0, rows, src] * inv
+                cover[b, :, dst] = wsum * inv
+
+        def go(i, carry):
+            s, b = i // owned, lax.rem(i, owned)
+            deblend(b, s * block + q * width, True)
+            return carry
+
+        lax.fori_loop(0, per_dest * owned, go, 0)
+
+    def ps_copy(it, d):
+        to = lax.rem(e + d, ne)
+        return pltpu.make_async_remote_copy(
+            src_ref=sums.at[it, 0], dst_ref=sums.at[it, d],
+            send_sem=ps_send.at[it, d - 1], recv_sem=ps_recv.at[it, d - 1],
+            device_id=(to, j), device_id_type=MESH,
+        )
+
+    def update(it):
+        packed = jnp.zeros((slots, LANES), f32)
+        for b in range(owned):
+            for c in range(bands + 1):
+                total_bc = jnp.sum(acc[b, c], axis=1, keepdims=True)
+                packed = jnp.where(lane == b * (bands + 1) + c, total_bc, packed)
+        sums[it, 0] = packed
+        for d in range(1, ne):
+            ps_copy(it, d).start()
+        for d in range(1, ne):
+            ps_copy(it, d).wait_recv()
+        whole = None
+        for o in range(ne):
+            slot = lax.rem(e - o + ne, ne)
+            v = sums[it, slot]
+            whole = v if whole is None else whole + v
+        for b in range(owned):
+            at = b * (bands + 1)
+            norm = whole[:, at + bands : at + bands + 1]
+            scale = 1.0 / (1.0 + count_ref[b].astype(f32) * norm)
+            for c in range(bands):
+                grad = jnp.broadcast_to(whole[:, at + c : at + c + 1] * scale, (slots, LANES))
+                by_band[b, c] = jnp.maximum(0.0, by_band[b, c] + grad)
+
+    acc[...] = jnp.zeros_like(acc)
+    for b in range(owned):
+        for c in range(bands):
+            by_band[b, c] = jnp.broadcast_to(spec_ref[b, :, c : c + 1], (slots, LANES))
+    spread()
+
+    local_sum(0)
+    pl.semaphore_wait(barrier, total - 1)
+    s1_start(0)
+    if chunks > 1:
+        local_sum(1)
+        s1_start(1)
+    for copy in side:
+        copy.wait()
+    for q in range(chunks + 2):
+        if q < chunks:
+            s2_start(q)
+        if q + 2 < chunks:
+            local_sum(q + 2)
+            s1_start(q + 2)
+        if 0 <= q - 1 < chunks:
+            s3_start(q - 1)
+        if 0 <= q - 2 < chunks:
+            finish(q - 2)
+
+    update(0)
+    spread()
+    for it in range(1, ITERS):
+        acc[...] = jnp.zeros_like(acc)
+
+        def again(i, carry):
+            w, b = i // owned, lax.rem(i, owned)
+            deblend(b, w * width, False)
+            return carry
+
+        lax.fori_loop(0, owned * (pix_part // width), again, 0)
+        update(it)
+        if it + 1 < ITERS:
+            spread()
+    for b in range(owned):
+        out = by_band[b, 0]
+        for c in range(1, bands):
+            out = jnp.where(lane == c, by_band[b, c], out)
+        spec_out[b] = out[:, :bands]
+
+    for q in range(chunks):
+        for a in range(2):
+            for d in range(1, line(a, True)[1]):
+                s1(a, q, d).wait_send()
+            for d in range(1, line(a, False)[1]):
+                s2(a, q, d).wait_send()
+
+        def sent(d, carry, q=q):
+            s3_remote(q, lax.rem(j + d, nb)).wait_send()
+            return carry
+
+        lax.fori_loop(1, nb, sent, 0)
+
+        @pl.when(jnp.logical_not(here))
+        def _(q=q):
+            s3_remote(q, j).wait_send()
+
+    for it in range(ITERS):
+        for d in range(1, ne):
+            ps_copy(it, d).wait_send()
+
+
+def fused(ne, nb, visit_flux, visit_precision, visit_live, footprint, source_count, spectra_init,
+          morphology_init):
+    visits, every_blend, bands, block = visit_flux.shape
+    owned, slots, pix_part = morphology_init.shape
+    ny, nx = factors(ne)
+    width = ne * LANES
+    chunks = block // width
+    per_dest = pix_part // block
+    rows = owned * bands
+    hop = max(nx, ny) - 1
+    f32 = jnp.float32
+    vmem, smem, hbm = (pl.BlockSpec(memory_space=s) for s in (pltpu.VMEM, pltpu.SMEM, pl.ANY))
+    dma = pltpu.SemaphoreType.DMA
+    return pl.pallas_call(
+        functools.partial(coadd_kernel, ne=ne, nb=nb, ny=ny, nx=nx),
+        out_shape=(
+            jax.ShapeDtypeStruct((owned, bands, pix_part), f32),
+            jax.ShapeDtypeStruct((owned, slots, bands), f32),
+            jax.ShapeDtypeStruct((owned, slots, pix_part), f32),
+        ),
+        in_specs=[hbm, hbm, smem, hbm, smem, vmem, hbm],
+        out_specs=(vmem, vmem, vmem),
+        scratch_shapes=[
+            pltpu.VMEM((chunks, visits, every_blend, bands, width), visit_flux.dtype),
+            pltpu.VMEM((chunks, visits, every_blend, bands, width), visit_precision.dtype),
+            pltpu.VMEM((owned, slots, pix_part), jnp.int32),
+            pltpu.VMEM((owned, bands, pix_part), f32),
+            pltpu.VMEM((2, chunks, ne, nb, rows, LANES), f32),
+            pltpu.VMEM((2, chunks, hop, max(nx, ny), nb, rows, LANES), f32),
+            pltpu.VMEM((2, chunks, max(nx, ny), nb, rows, LANES), f32),
+            pltpu.VMEM((2, chunks, hop, nb, rows, LANES), f32),
+            pltpu.VMEM((chunks, nb, 2, rows, LANES), f32),
+            pltpu.VMEM((chunks, 2, rows, per_dest * width), f32),
+            pltpu.VMEM((owned, bands, slots, LANES), f32),
+            pltpu.VMEM((owned, slots, bands, LANES), f32),
+            pltpu.VMEM((owned, slots, LANES), f32),
+            pltpu.VMEM((owned, bands + 1, slots, LANES), f32),
+            pltpu.VMEM((ITERS, ne, slots, LANES), f32),
+            dma((2, chunks)),
+            dma((2,)),
+            dma((2, chunks, hop)),
+            dma((2, chunks, hop)),
+            dma((2, chunks, hop)),
+            dma((2, chunks, hop)),
+            dma((chunks, nb)),
+            dma((chunks,)),
+            dma((ITERS, ne - 1)),
+            dma((ITERS, ne - 1)),
+        ],
+        compiler_params=pltpu.CompilerParams(
+            collective_id=0, has_side_effects=True, vmem_limit_bytes=56 * 2**20
+        ),
+    )(visit_flux, visit_precision, visit_live, footprint, source_count, spectra_init,
+      morphology_init)
 
 
 def on_device(
@@ -65,6 +480,23 @@
 
 
 def solution(mesh):
+    ne, nb = mesh.shape["epoch"], mesh.shape["blend"]
+
+    def step(visit_flux, visit_precision, visit_live, footprint, source_count, spectra_init,
+             morphology_init):
+        block, bands = visit_flux.shape[3], visit_flux.shape[2]
+        owned, pix_part = morphology_init.shape[0], morphology_init.shape[2]
+        ny, nx = factors(ne)
+        fits = (
+            block % (ne * LANES) == 0
+            and pix_part % block == 0
+            and min(ny, nx) > 1
+            and owned * (bands + 1) <= LANES
+        )
+        run = functools.partial(fused, ne, nb) if fits else on_device
+        return run(visit_flux, visit_precision, visit_live, footprint, source_count, spectra_init,
+                   morphology_init)
+
     in_specs = (
         P("epoch", None, None, "blend"),
         P("epoch", None, None, "blend"),
@@ -76,5 +508,5 @@
     )
     out_specs = (P("blend", None, "epoch"), P("blend", None, None), P("blend", None, "epoch"))
     return jax.shard_map(
-        on_device, mesh=mesh, in_specs=in_specs, out_specs=out_specs, check_vma=False
-    )
+        step, mesh=mesh, in_specs=in_specs, out_specs=out_specs, check_vma=False
+    )

time: 168 us -> 78 us (0.46)
  waiting for transfers between devices: 83.4 us -> 0 us
  Pallas kernels: 0 us -> 60.6 us
  blocking collectives: 30.4 us -> 0 us
  starting transfers between devices: 16.2 us -> 0 us
  between operations: 14.2 us -> 0.65 us
  other arithmetic: 7.82 us -> 0 us
  local copies, waits for them, and re-layouts: 8.92 us -> 16.3 us
  matrix products: 6.48 us -> 0 us
    reduce_scatter x2 -> x0, waiting for transfers between devices: 60.7 us -> none  [the longest x1 33.3 us: on_device(): lax.psum_scatter(weight_sum, 'epoch', scatter_dimension=2, tiled=True)]
    pallas_call x0 -> x1, Pallas kernels: none -> 60.6 us  [fused(): pl.pallas_call(functools.partial(coadd_kernel, ne=ne, nb=nb, ny=ny, nx=nx...]
    psum x2 -> x0, blocking collectives: 30.4 us -> none  [on_device(): spectra_grad, morph_norm = lax.psum((spectra_grad, morph_norm), 'epoch')]
    all_to_all x4 -> x0, waiting for transfers between devices: 22 us -> none  [the longest x1 11.7 us: on_device(): lax.all_to_all(numerator, 'blend', split_axis=0, concat_axis=2, tiled=True)]
    all_to_all x4 -> x0, starting transfers between devices: 16.1 us -> none  [the longest x1 4.59 us: on_device(): lax.all_to_all(weight_sum, 'blend', split_axis=0, concat_axis=2, tiled=True)]
    unnamed x13 -> x6, local copies, waits for them, and re-layouts: 1.82 us -> 12.9 us
    reduce_sum x3 -> x0, other arithmetic: 6.6 us -> none  [the longest x1 6.42 us: on_device(): weight_sum = jnp.sum(weights, axis=0)]
    dot_general x8 -> x0, matrix products: 6.48 us -> none  [the longest x4 2.63 us: on_device(): jnp.einsum('bkc,bkp->bcp', spectra, morphology, precision=highest)]
  transfers between devices with their start and end apart: 6 -> 0, of which waited for: 5 -> 0; matrix products, arithmetic and copies ran while one was open for 4% -> 0% of each run, Pallas kernels for 0% -> 0%
where the time goes in v1:
time: 78 us; the launch traced here: 77.5 us
  Pallas kernels  60.6 us (78%)
  local copies, waits for them, and re-layouts  16.3 us (21%)
    pallas_call x1, Pallas kernels, fused(): pl.pallas_call(functools.partial(coadd_kernel, ne=ne, nb=nb, ny=ny, nx=nx...  60.6 us
    unnamed x6, local copies, waits for them, and re-layouts  12.9 us
    pallas_call x2, local copies, waits for them, and re-layouts, fused(): pl.pallas_call(functools.partial(coadd_kernel, ne=ne, nb=nb, ny=ny, nx=nx...  3.45 us

profile of v1, /device:TPU:0, one launch (start us, length us, event | category | flops | bytes accessed | tf_op | source)
XLA Modules:
  0.0 77.5 jit_solution(15745909960553832944)
XLA Ops:
  0.6 0.0 copy-start
  0.6 1.6 %copy.12.spec_ref = f32[4,8,6]{2,1,0:T(8,128)} copy(f32[4,8,6]{1,0,2:T(4,128)} %param.12) | data formatting | bytes 1536 | tf_op args[5]
  2.2 5.7 %copy.10.flux_hbm = bf16[4,32,6,2048]{3,2,1,0:T(8,128)(2,1)} copy(bf16[4,32,6,2048]{3,1,2,0:T(8,128)(2,1)} %param.7) | data formatting | bytes 6291456 | tf_op args[0]
  7.9 0.0 copy-done
  7.9 3.7 %copy.11.prec_hbm = bf16[4,32,6,2048]{3,2,1,0:T(8,128)(2,1)} copy(bf16[4,32,6,2048]{3,1,2,0:T(8,128)(2,1)S(1)} %copy-done) | data formatting | bytes 6291456 | tf_op args[1]
  11.6 60.6 %shard_map.94 = (f32[4,6,4096]{2,1,0:T(8,128)}, f32[4,8,6]{2,1,0:T(8,128)}, f32[4,8,4096]{2,1,0:T(8,128)}) custom-call(bf16[4,32,6,2048]{3,2,1,0:T(8,128)(2,1)} %copy.10.flux_hbm, bf16[4,32,6,2048]{3,2,1,0:T(8,128)(2,1)} %copy.11.prec_hbm, s32[4,32]{1,0:T(4,128)} %live_ref.1, s32[4,8,4096]{2,1,0:T(8,128)} %foot_hbm.1, s32[4]{0:T(128)} %count_ref.1, ...), custom_call_target="tpu_custom_call" | custom-call | tf_op jit(solution)/shard_map/pallas_call | solution.py:381
  72.2 2.0 %copy.13 = f32[4,6,4096]{2,0,1:T(4,128)} copy(f32[4,6,4096]{2,1,0:T(8,128)} %get-tuple-element.3) | data formatting | bytes 786432 | tf_op jit(solution)/shard_map/pallas_call | solution.py:381
  74.3 1.4 %copy.14 = f32[4,8,6]{1,0,2:T(4,128)} copy(f32[4,8,6]{2,1,0:T(8,128)} %get-tuple-element.4) | data formatting | bytes 1536 | tf_op jit(solution)/shard_map/pallas_call | solution.py:381
  75.7 1.9 %copy.16 = f32[4,8,4096]{2,1,0:T(8,128)} copy(f32[4,8,4096]{2,1,0:T(8,128)} %get-tuple-element.11) | data formatting | bytes 1048576
Async XLA Ops:
  0.6 7.3 %copy-start = (bf16[4,32,6,2048]{3,1,2,0:T(8,128)(2,1)S(1)}, bf16[4,32,6,2048]{3,1,2,0:T(8,128)(2,1)}, u32[]{:S(2)}) copy-start(bf16[4,32,6,2048]{3,1,2,0:T(8,128)(2,1)} %param.8) | copy-start | bytes 9437188

commit v2 on v1

v2 whole, which is shorter than its diff:
```python
import functools

import jax
import jax.numpy as jnp
from jax import lax
from jax.experimental import pallas as pl
from jax.experimental.pallas import tpu as pltpu
from jax.sharding import PartitionSpec as P

ITERS = 2


LANES = 128
MESH = pl.DeviceIdType.MESH


def factors(count):
    rows = max(d for d in range(1, count + 1) if count % d == 0 and d * d <= count)
    return rows, count // rows


def coadd_kernel(
    flux_hbm, prec_hbm, live_ref, foot_hbm, count_ref, spec_ref, morph_hbm,
    coadd_ref, spec_out, morph_ref,
    flux_v, prec_v, foot_v, flux_c, cover,
    stage, land1, part, land2, final, pieces, spectra, step_ref, acc, sums,
    in_sem, side_sem, s1_send, s1_recv, s2_send, s2_recv, s3_send, s3_recv, ps_send, ps_recv,
    *, ne, nb, ny, nx,
):
    visits, bands, every_blend, block = flux_hbm.shape
    owned, slots, pix_part = morph_hbm.shape
    chunks = flux_v.shape[0]
    width = block // chunks
    per_dest = pix_part // block
    held = per_dest * owned
    e = lax.axis_index("epoch")
    j = lax.axis_index("blend")
    y, x = e // nx, e % nx
    home_e = j // per_dest
    home_slot = j % per_dest
    f32 = jnp.float32

    def in_copy(q):
        window = pl.ds(q * width, width)
        return (
            pltpu.make_async_copy(prec_hbm.at[:, :, :, window], prec_v.at[q], in_sem.at[0, q]),
            pltpu.make_async_copy(flux_hbm.at[:, :, :, window], flux_v.at[q], in_sem.at[1, q]),
        )

    side = []
    for s in range(per_dest):
        for b in range(owned):
            row = s * owned + b
            window = pl.ds(s * block, block)
            side.append(pltpu.make_async_copy(
                foot_hbm.at[b, :, window], foot_v.at[:, row, :], side_sem.at[0, row]))
            side.append(pltpu.make_async_copy(
                morph_hbm.at[b, :, window], morph_ref.at[:, row, :], side_sem.at[1, row]))

    for q in range(chunks):
        for copy in in_copy(q):
            copy.start()

    barrier = pltpu.get_barrier_semaphore()
    total = ne * nb
    mine = e * nb + j

    def greet(d, carry):
        other = lax.rem(mine + d, total)
        pl.semaphore_signal(
            barrier, inc=1, device_id=(other // nb, lax.rem(other, nb)), device_id_type=MESH
        )
        return carry

    lax.fori_loop(1, total, greet, 0)

    square_r = lax.broadcasted_iota(jnp.int32, (every_blend, every_blend), 0)
    square_c = lax.broadcasted_iota(jnp.int32, (every_blend, every_blend), 1)
    lives = []
    for v in range(visits):
        row = jnp.broadcast_to(live_ref[v : v + 1, :].astype(f32), (every_blend, every_blend))
        column = jnp.sum(jnp.where(square_r == square_c, row, 0.0), axis=1, keepdims=True)
        lives.append(jnp.broadcast_to(column, (every_blend, LANES)))

    def local_sum(q):
        for copy in in_copy(q):
            copy.wait()

        def one(c, carry):
            for p in range(ne):
                lanes = slice(p * LANES, (p + 1) * LANES)
                py, px = p // nx, p % nx
                num = None
                for v in range(visits):
                    w = prec_v[q, v, c, :, lanes].astype(f32) * lives[v]
                    n = w * flux_v[q, v, c, :, lanes].astype(f32)
                    num, wsum = (n, w) if num is None else (num + n, wsum + w)
                stage[0, q, px * ny + py, c] = num
                stage[1, q, py * nx + px, c] = wsum
            return carry

        lax.fori_loop(0, bands, one, 0)

    def line(a, first):
        along_x = (a == 0) == first
        return (x, nx) if along_x else (y, ny)

    def device_at(a, first, where):
        along_x = (a == 0) == first
        return (y * nx + where if along_x else where * nx + x, j)

    def s1(a, q, d):
        at, n = line(a, True)
        other = line(a, False)[1]
        to = lax.rem(at + d, n)
        return pltpu.make_async_remote_copy(
            src_ref=stage.at[a, q, pl.ds(to * other, other)],
            dst_ref=land1.at[a, q, d - 1],
            send_sem=s1_send.at[a, q, d - 1], recv_sem=s1_recv.at[a, q, d - 1],
            device_id=device_at(a, True, to), device_id_type=MESH,
        )

    def s2(a, q, d):
        at, n = line(a, False)
        to = lax.rem(at + d, n)
        return pltpu.make_async_remote_copy(
            src_ref=part.at[a, q, to],
            dst_ref=land2.at[a, q, d - 1],
            send_sem=s2_send.at[a, q, d - 1], recv_sem=s2_recv.at[a, q, d - 1],
            device_id=device_at(a, False, to), device_id_type=MESH,
        )

    def s1_start(q):
        for a in range(2):
            for d in range(1, line(a, True)[1]):
                s1(a, q, d).start()

    def s2_start(q):
        for a in range(2):
            at, n = line(a, True)
            others = line(a, False)[1]
            for d in range(1, n):
                s1(a, q, d).wait_recv()

            def add(c, carry):
                for o in range(others):
                    v = stage[a, q, at * others + o, c]
                    for d in range(1, n):
                        v = v + land1[a, q, d - 1, o, c]
                    part[a, q, o, c] = v
                return carry

            lax.fori_loop(0, bands, add, 0)
            for d in range(1, others):
                s2(a, q, d).start()

    here = home_e == e

    def landing(q):
        lanes = pl.ds(pl.multiple_of(e * LANES, LANES), LANES)
        return pieces.at[q, :, :, home_slot, :, lanes]

    def s3_local(q):
        return pltpu.make_async_copy(final.at[q, j], landing(q), s3_recv.at[q])

    def s3_remote(q, to):
        return pltpu.make_async_remote_copy(
            src_ref=final.at[q, to], dst_ref=landing(q),
            send_sem=s3_send.at[q, to], recv_sem=s3_recv.at[q],
            device_id=(home_e, to), device_id_type=MESH,
        )

    def s3_start(q):
        for a in range(2):
            at, n = line(a, False)
            for d in range(1, n):
                s2(a, q, d).wait_recv()

            def add(c, carry):
                v = part[a, q, at, c]
                for d in range(1, n):
                    v = v + land2[a, q, d - 1, c]
                for to in range(nb):
                    final[q, to, a, c] = v[to * owned : (to + 1) * owned, :]
                return carry

            lax.fori_loop(0, bands, add, 0)

        def send(d, carry):
            s3_remote(q, lax.rem(j + d, nb)).start()
            return carry

        lax.fori_loop(1, nb, send, 0)

        @pl.when(here)
        def _():
            s3_local(q).start()

        @pl.when(jnp.logical_not(here))
        def _():
            s3_remote(q, j).start()

    sub = lax.broadcasted_iota(jnp.int32, (held, LANES), 0)
    lane = lax.broadcasted_iota(jnp.int32, (held, LANES), 1)
    count = jnp.zeros((held, LANES), jnp.int32)
    for b in range(owned):
        count = jnp.where(lax.rem(sub, owned) == b, count_ref[b], count)
    live_count = count.astype(f32)

    def steps():
        for k in range(slots):
            norm = None
            for c in range(bands):
                s = spectra[k, c]
                norm = s * s if norm is None else norm + s * s
            step_ref[k] = 1.0 / (1.0 + live_count * norm)

    group = 2

    def deblend(start, first):
        runs = [
            pl.ds(pl.multiple_of(start + t * LANES, LANES), LANES) for t in range(group)
        ]

        def masks(k):
            live = jnp.where(count > k, 1.0, 0.0).astype(f32)
            return [foot_v[k, :, px].astype(f32) * live for px in runs]

        def residual(morph):
            res = []
            for c in range(bands):
                model = [None] * group
                for k in range(slots):
                    s = spectra[k, c]
                    for t in range(group):
                        v = s * morph[k][t]
                        model[t] = v if k == 0 else model[t] + v
                res.append([
                    cover[c, :, px] * (flux_c[c, :, px] - model[t]) for t, px in enumerate(runs)
                ])
            return res

        morph = []
        for k in range(slots):
            m = [morph_ref[k, :, px] for px in runs]
            morph.append([a * b for a, b in zip(m, masks(k))] if first else m)
        res = residual(morph)
        for k in range(slots):
            mask = masks(k)
            grad = [None] * group
            for c in range(bands):
                s = spectra[k, c]
                for t in range(group):
                    v = s * res[c][t]
                    grad[t] = v if c == 0 else grad[t] + v
            step = step_ref[k]
            for t, px in enumerate(runs):
                m = jnp.maximum(0.0, morph[k][t] + grad[t] * step) * mask[t]
                morph[k][t] = m
                morph_ref[k, :, px] = m
        res = residual(morph)
        for k in range(slots):
            for c in range(bands):
                v = acc[k, c]
                for t in range(group):
                    v = v + morph[k][t] * res[c][t]
                acc[k, c] = v
            v = acc[k, bands]
            for t in range(group):
                v = v + morph[k][t] * morph[k][t]
            acc[k, bands] = v

    def finish(q):
        pltpu.make_async_copy(pieces.at[q], pieces.at[q], s3_recv.at[q]).wait()
        at = slice(q * width, (q + 1) * width)

        def unpack(c, carry):
            for s in range(per_dest):
                rows = slice(s * owned, (s + 1) * owned)
                wsum = pieces[q, 1, c, s]
                inv = 1.0 / (1.0 + wsum)
                flux = pieces[q, 0, c, s] * inv
                coadd_ref[c, :, s * block + q * width : s * block + (q + 1) * width] = flux
                flux_c[c, rows, at] = flux
                cover[c, rows, at] = wsum * inv
            return carry

        lax.fori_loop(0, bands, unpack, 0)

        def go(i, carry):
            deblend(q * width + i * (group * LANES), True)
            return carry

        lax.fori_loop(0, width // (group * LANES), go, 0)

    def ps_copy(it, d):
        to = lax.rem(e + d, ne)
        return pltpu.make_async_remote_copy(
            src_ref=sums.at[it, 0], dst_ref=sums.at[it, d],
            send_sem=ps_send.at[it, d - 1], recv_sem=ps_recv.at[it, d - 1],
            device_id=(to, j), device_id_type=MESH,
        )

    def update(it):
        packed = jnp.zeros((held, LANES), f32)
        for k in range(slots):
            for c in range(bands + 1):
                whole = jnp.sum(acc[k, c], axis=1, keepdims=True)
                packed = jnp.where(lane == k * (bands + 1) + c, whole, packed)
        sums[it, 0] = packed
        for d in range(1, ne):
            ps_copy(it, d).start()
        for d in range(1, ne):
            ps_copy(it, d).wait_recv()
        whole = None
        for o in range(ne):
            v = sums[it, lax.rem(e - o + ne, ne)]
            whole = v if whole is None else whole + v
        one = whole[0:owned, :]
        for s in range(1, per_dest):
            one = one + whole[s * owned : (s + 1) * owned, :]
        whole = jnp.concatenate([one] * per_dest, axis=0)
        for k in range(slots):
            at = k * (bands + 1)
            norm = jnp.broadcast_to(whole[:, at + bands : at + bands + 1], (held, LANES))
            scale = 1.0 / (1.0 + live_count * norm)
            for c in range(bands):
                grad = jnp.broadcast_to(whole[:, at + c : at + c + 1], (held, LANES))
                spectra[k, c] = jnp.maximum(0.0, spectra[k, c] + grad * scale)

    local_sum(0)
    pl.semaphore_wait(barrier, total - 1)
    s1_start(0)
    if chunks > 1:
        local_sum(1)
        s1_start(1)
    for copy in side:
        copy.start()

    acc[...] = jnp.zeros_like(acc)
    for k in range(slots):
        for c in range(bands):
            start = jnp.broadcast_to(spec_ref[c, :, k : k + 1], (owned, LANES))
            spectra[k, c] = jnp.concatenate([start] * per_dest, axis=0)
    steps()

    for q in range(chunks + 2):
        if q < chunks:
            s2_start(q)
        if q + 2 < chunks:
            local_sum(q + 2)
            s1_start(q + 2)
        if 0 <= q - 1 < chunks:
            s3_start(q - 1)
        if q == 2:
            for copy in side:
                copy.wait()
        if 0 <= q - 2 < chunks:
            finish(q - 2)

    update(0)
    for it in range(1, ITERS):
        steps()
        acc[...] = jnp.zeros_like(acc)

        def again(i, carry):
            deblend(i * (group * LANES), False)
            return carry

        lax.fori_loop(0, block // (group * LANES), again, 0)
        update(it)
    for c in range(bands):
        out = spectra[0, c]
        for k in range(1, slots):
            out = jnp.where(lane == k, spectra[k, c], out)
        spec_out[c] = out[0:owned, :slots]

    for q in range(chunks):
        for a in range(2):
            for d in range(1, line(a, True)[1]):
                s1(a, q, d).wait_send()
            for d in range(1, line(a, False)[1]):
                s2(a, q, d).wait_send()

        def sent(d, carry, q=q):
            s3_remote(q, lax.rem(j + d, nb)).wait_send()
            return carry

        lax.fori_loop(1, nb, sent, 0)

        @pl.when(jnp.logical_not(here))
        def _(q=q):
            s3_remote(q, j).wait_send()

    for it in range(ITERS):
        for d in range(1, ne):
            ps_copy(it, d).wait_send()


def hand_over(coadd_in, spec_in, morph_in, coadd_out, spec_out, morph_out, sems, row_sems):
    owned, _, pix_part = morph_out.shape
    _, held, block = morph_in.shape
    copies = [
        pltpu.make_async_copy(morph_in.at[:, row, :],
                              morph_out.at[row % owned, :, pl.ds(row // owned * block, block)],
                              row_sems.at[row])
        for row in range(held)
    ]
    copies.append(pltpu.make_async_copy(coadd_in, coadd_out, sems.at[0]))
    copies.append(pltpu.make_async_copy(spec_in, spec_out, sems.at[1]))
    for copy in copies:
        copy.start()
    for copy in copies:
        copy.wait()


def fused(ne, nb, visit_flux, visit_precision, visit_live, footprint, source_count, spectra_init,
          morphology_init):
    visits, every_blend, bands, block = visit_flux.shape
    owned, slots, pix_part = morphology_init.shape
    ny, nx = factors(ne)
    width = ne * LANES
    chunks = block // width
    per_dest = pix_part // block
    held = per_dest * owned
    hop = max(nx, ny) - 1
    line = max(nx, ny)
    f32 = jnp.float32
    vmem, smem, hbm = (pl.BlockSpec(memory_space=s) for s in (pltpu.VMEM, pltpu.SMEM, pl.ANY))
    dma = pltpu.SemaphoreType.DMA
    parts = pl.pallas_call(
        functools.partial(coadd_kernel, ne=ne, nb=nb, ny=ny, nx=nx),
        out_shape=(
            jax.ShapeDtypeStruct((bands, owned, pix_part), f32),
            jax.ShapeDtypeStruct((bands, owned, slots), f32),
            jax.ShapeDtypeStruct((slots, held, block), f32),
        ),
        in_specs=[hbm, hbm, vmem, hbm, smem, vmem, hbm],
        out_specs=(vmem, vmem, vmem),
        scratch_shapes=[
            pltpu.VMEM((chunks, visits, bands, every_blend, width), visit_flux.dtype),
            pltpu.VMEM((chunks, visits, bands, every_blend, width), visit_precision.dtype),
            pltpu.VMEM((slots, held, block), jnp.int32),
            pltpu.VMEM((bands, held, block), f32),
            pltpu.VMEM((bands, held, block), f32),
            pltpu.VMEM((2, chunks, ne, bands, every_blend, LANES), f32),
            pltpu.VMEM((2, chunks, hop, line, bands, every_blend, LANES), f32),
            pltpu.VMEM((2, chunks, line, bands, every_blend, LANES), f32),
            pltpu.VMEM((2, chunks, hop, bands, every_blend, LANES), f32),
            pltpu.VMEM((chunks, nb, 2, bands, owned, LANES), f32),
            pltpu.VMEM((chunks, 2, bands, per_dest, owned, width), f32),
            pltpu.VMEM((slots, bands, held, LANES), f32),
            pltpu.VMEM((slots, held, LANES), f32),
            pltpu.VMEM((slots, bands + 1, held, LANES), f32),
            pltpu.VMEM((ITERS, ne, held, LANES), f32),
            dma((2, chunks)),
            dma((2, held)),
            dma((2, chunks, hop)),
            dma((2, chunks, hop)),
            dma((2, chunks, hop)),
            dma((2, chunks, hop)),
            dma((chunks, nb)),
            dma((chunks,)),
            dma((ITERS, ne - 1)),
            dma((ITERS, ne - 1)),
        ],
        compiler_params=pltpu.CompilerParams(
            collective_id=0, has_side_effects=True, vmem_limit_bytes=62 * 2**20
        ),
    )(visit_flux.transpose(0, 2, 1, 3), visit_precision.transpose(0, 2, 1, 3), visit_live,
      footprint, source_count, spectra_init.transpose(2, 0, 1), morphology_init)
    coadd, spectra, morphology = pl.pallas_call(
        hand_over,
        out_shape=(
            jax.ShapeDtypeStruct((bands, owned, pix_part), f32),
            jax.ShapeDtypeStruct((bands, owned, slots), f32),
            jax.ShapeDtypeStruct((owned, slots, pix_part), f32),
        ),
        in_specs=[vmem] * 3,
        out_specs=(hbm,) * 3,
        scratch_shapes=[dma((2,)), dma((held,))],
        compiler_params=pltpu.CompilerParams(vmem_limit_bytes=8 * 2**20),
    )(*parts)
    return coadd.transpose(1, 0, 2), spectra.transpose(1, 2, 0), morphology


def on_device(
    visit_flux, visit_precision, visit_live, footprint, source_count, spectra_init, morphology_init
):
    weights = visit_precision.astype(jnp.float32) * visit_live.astype(jnp.float32)[:, :, None, None]
    numerator = jnp.sum(weights * visit_flux.astype(jnp.float32), axis=0)
    weight_sum = jnp.sum(weights, axis=0)
    pix_part = morphology_init.shape[2]
    owned = morphology_init.shape[0]
    numerator, weight_sum = (
        lax.psum_scatter(numerator, "epoch", scatter_dimension=2, tiled=True),
        lax.psum_scatter(weight_sum, "epoch", scatter_dimension=2, tiled=True),
    )
    every_blend, band_count, piece = numerator.shape
    numerator = numerator.reshape(every_blend, band_count, 1, piece)
    weight_sum = weight_sum.reshape(every_blend, band_count, 1, piece)
    numerator, weight_sum = (
        lax.all_to_all(numerator, "blend", split_axis=0, concat_axis=2, tiled=True),
        lax.all_to_all(weight_sum, "blend", split_axis=0, concat_axis=2, tiled=True),
    )
    blocks = numerator.shape[2]
    numerator = numerator.reshape(owned, band_count, blocks, 1, piece)
    weight_sum = weight_sum.reshape(owned, band_count, blocks, 1, piece)
    numerator, weight_sum = (
        lax.all_to_all(numerator, "epoch", split_axis=2, concat_axis=3, tiled=True),
        lax.all_to_all(weight_sum, "epoch", split_axis=2, concat_axis=3, tiled=True),
    )
    numerator = numerator.reshape(owned, band_count, pix_part)
    weight_sum = weight_sum.reshape(owned, band_count, pix_part)
    coadd_flux = numerator / (1.0 + weight_sum)
    coverage = weight_sum / (1.0 + weight_sum)
    slots = footprint.shape[1]
    source_live = (jnp.arange(slots, dtype=jnp.int32)[None, :] < source_count[:, None]).astype(
        jnp.float32
    )
    footprint_mask = footprint.astype(jnp.float32) * source_live[:, :, None]
    live_count = source_count.astype(jnp.float32)
    morphology = morphology_init * footprint_mask
    spectra = spectra_init
    highest = lax.Precision.HIGHEST
    for iteration in range(ITERS):
        blend_model = jnp.einsum("bkc,bkp->bcp", spectra, morphology, precision=highest)
        residual = coverage * (coadd_flux - blend_model)
        morph_grad = jnp.einsum("bkc,bcp->bkp", spectra, residual, precision=highest)
        morph_step = 1.0 / (1.0 + live_count[:, None] * jnp.sum(spectra * spectra, axis=2))
        morphology = (
            jnp.maximum(0.0, morphology + morph_grad * morph_step[:, :, None]) * footprint_mask
        )
        blend_model = jnp.einsum("bkc,bkp->bcp", spectra, morphology, precision=highest)
        residual = coverage * (coadd_flux - blend_model)
        spectra_grad = jnp.einsum("bkp,bcp->bkc", morphology, residual, precision=highest)
        morph_norm = jnp.sum(morphology * morphology, axis=2)
        spectra_grad, morph_norm = lax.psum((spectra_grad, morph_norm), "epoch")
        spectra = jnp.maximum(
            0.0, spectra + spectra_grad / (1.0 + live_count[:, None] * morph_norm)[:, :, None]
        )
    return (coadd_flux, spectra, morphology)


def solution(mesh):
    ne, nb = mesh.shape["epoch"], mesh.shape["blend"]

    def step(visit_flux, visit_precision, visit_live, footprint, source_count, spectra_init,
             morphology_init):
        block, bands = visit_flux.shape[3], visit_flux.shape[2]
        owned, pix_part = morphology_init.shape[0], morphology_init.shape[2]
        ny, nx = factors(ne)
        fits = (
            block % (ne * LANES) == 0
            and pix_part % block == 0
            and min(ny, nx) > 1
            and morphology_init.shape[1] * (bands + 1) <= LANES
        )
        run = functools.partial(fused, ne, nb) if fits else on_device
        return run(visit_flux, visit_precision, visit_live, footprint, source_count, spectra_init,
                   morphology_init)

    in_specs = (
        P("epoch", None, None, "blend"),
        P("epoch", None, None, "blend"),
        P("epoch", None),
        P("blend", None, "epoch"),
        P("blend"),
        P("blend", None, None),
        P("blend", None, "epoch"),
    )
    out_specs = (P("blend", None, "epoch"), P("blend", None, None), P("blend", None, "epoch"))
    return jax.shard_map(
        step, mesh=mesh, in_specs=in_specs, out_specs=out_specs, check_vma=False
    )
```

time: 78 us -> 61.4 us (0.79)
  local copies, waits for them, and re-layouts: 16.3 us -> 2.74 us
  Pallas kernels: 60.6 us -> 57.7 us
    unnamed x6, local copies, waits for them, and re-layouts: 12.9 us -> 2.74 us
    pallas_call x1, Pallas kernels: 60.6 us -> 56.7 us  [fused(): pl.pallas_call(functools.partial(coadd_kernel, ne=ne, nb=nb, ny=ny, nx=nx...]
    pallas_call x2 -> x0, local copies, waits for them, and re-layouts: 3.45 us -> none  [fused(): pl.pallas_call(functools.partial(coadd_kernel, ne=ne, nb=nb, ny=ny, nx=nx...]
    pallas_call x0 -> x1, Pallas kernels: none -> 1 us  [fused(): pl.pallas_call(hand_over, out_shape=(jax.ShapeDtypeStruct((bands, owned,...]
where the time goes in v2:
time: 61.4 us; the launch traced here: 61.1 us
  Pallas kernels  57.7 us (94%)
  local copies, waits for them, and re-layouts  2.74 us (4%)
  between operations  0.65 us (1%)
    pallas_call x1, Pallas kernels, fused(): pl.pallas_call(functools.partial(coadd_kernel, ne=ne, nb=nb, ny=ny, nx=nx...  56.7 us
    unnamed x6, local copies, waits for them, and re-layouts  2.74 us

profile of v2, /device:TPU:0, one launch (start us, length us, event | category | flops | bytes accessed | tf_op | source)
XLA Modules:
  0.0 61.1 jit_solution(17372471432649171431)
XLA Ops:
  0.6 56.7 %shard_map.94 = (f32[6,4,4096]{2,1,0:T(4,128)}, f32[6,4,8]{2,1,0:T(4,128)}, f32[8,8,2048]{2,1,0:T(8,128)}) custom-call(bf16[4,6,32,2048]{3,2,1,0:T(8,128)(2,1)} %bitcast.5, bf16[4,6,32,2048]{3,2,1,0:T(8,128)(2,1)} %bitcast.6, s32[4,32]{1,0:T(4,128)} %live_ref.1, s32[4,8,4096]{2,1,0:T(8,128)} %foot_hbm.1, s32[4]{0:T(128)} %count_ref.1, f32[6,4,8]{2,1,0:T(4,128)} %bitcast.7, ...), custom_call_target="tpu_custom_call" | custom-call | tf_op jit(solution)/shard_map/pallas_call | solution.py:431
  57.3 0.0 copy-start
  57.4 1.0 %copy-done = f32[8,8,2048]{2,1,0:T(8,128)S(1)} copy-done((f32[8,8,2048]{2,1,0:T(8,128)S(1)}, f32[8,8,2048]{2,1,0:T(8,128)}, u32[]{:S(2)}) %copy-start) | copy-done | bytes 524312
  58.4 0.0 copy-start.1
  58.4 1.0 %copy-done.1 = f32[6,4,4096]{2,1,0:T(4,128)S(1)} copy-done((f32[6,4,4096]{2,1,0:T(4,128)S(1)}, f32[6,4,4096]{2,1,0:T(4,128)}, u32[]{:S(2)}) %copy-start.1) | copy-done | bytes 393240
  59.4 0.0 copy-start.2
  59.4 0.7 %copy-done.2 = f32[6,4,8]{2,1,0:T(4,128)S(1)} copy-done((f32[6,4,8]{2,1,0:T(4,128)S(1)}, f32[6,4,8]{2,1,0:T(4,128)}, u32[]{:S(2)}) %copy-start.2) | copy-done | bytes 792
  60.1 1.0 %shard_map.95 = (f32[6,4,4096]{2,1,0:T(4,128)}, f32[6,4,8]{2,1,0:T(4,128)}, f32[4,8,4096]{2,1,0:T(8,128)}) custom-call(f32[6,4,4096]{2,1,0:T(4,128)S(1)} %copy-done.1, f32[6,4,8]{2,1,0:T(4,128)S(1)} %copy-done.2, f32[8,8,2048]{2,1,0:T(8,128)S(1)} %copy-done), custom_call_target="tpu_custom_call" | custom-call | tf_op jit(solution)/shard_map/pallas_call | solution.py:472
Async XLA Ops:
  57.3 1.0 %copy-start = (f32[8,8,2048]{2,1,0:T(8,128)S(1)}, f32[8,8,2048]{2,1,0:T(8,128)}, u32[]{:S(2)}) copy-start(f32[8,8,2048]{2,1,0:T(8,128)} %get-tuple-element.11.morph_in) | copy-start | bytes 1572868
  58.4 1.0 %copy-start.1 = (f32[6,4,4096]{2,1,0:T(4,128)S(1)}, f32[6,4,4096]{2,1,0:T(4,128)}, u32[]{:S(2)}) copy-start(f32[6,4,4096]{2,1,0:T(4,128)} %get-tuple-element.9.coadd_in) | copy-start | bytes 1179652
  59.4 0.7 %copy-start.2 = (f32[6,4,8]{2,1,0:T(4,128)S(1)}, f32[6,4,8]{2,1,0:T(4,128)}, u32[]{:S(2)}) copy-start(f32[6,4,8]{2,1,0:T(4,128)} %get-tuple-element.10.spec_in) | copy-start | bytes 2308

commit v3 on v2

--- a/solution.py
+++ b/solution.py
@@ -8,6 +8,7 @@
 from jax.sharding import PartitionSpec as P
 
 ITERS = 2
+AHEAD = 3
 
 
 LANES = 128
@@ -23,8 +24,8 @@
     flux_hbm, prec_hbm, live_ref, foot_hbm, count_ref, spec_ref, morph_hbm,
     coadd_ref, spec_out, morph_ref,
     flux_v, prec_v, foot_v, flux_c, cover,
-    stage, land1, part, land2, final, pieces, spectra, step_ref, acc, sums,
-    in_sem, side_sem, s1_send, s1_recv, s2_send, s2_recv, s3_send, s3_recv, ps_send, ps_recv,
+    stage, land1, part, land2, final, column, pieces, spectra, step_ref, acc, sums,
+    in_sem, side_sem, s1_send, s1_recv, s2_send, s2_recv, s3_send, s3_recv, s4_send, s4_recv, ps_send, ps_recv,
     *, ne, nb, ny, nx,
 ):
     visits, bands, every_blend, block = flux_hbm.shape
@@ -33,11 +34,12 @@
     width = block // chunks
     per_dest = pix_part // block
     held = per_dest * owned
+    cuts = final.shape[0] // chunks
+    some = bands // cuts
+    units = chunks * cuts
     e = lax.axis_index("epoch")
     j = lax.axis_index("blend")
     y, x = e // nx, e % nx
-    home_e = j // per_dest
-    home_slot = j % per_dest
     f32 = jnp.float32
 
     def in_copy(q):
@@ -79,12 +81,17 @@
     lives = []
     for v in range(visits):
         row = jnp.broadcast_to(live_ref[v : v + 1, :].astype(f32), (every_blend, every_blend))
-        column = jnp.sum(jnp.where(square_r == square_c, row, 0.0), axis=1, keepdims=True)
-        lives.append(jnp.broadcast_to(column, (every_blend, LANES)))
-
-    def local_sum(q):
-        for copy in in_copy(q):
-            copy.wait()
+        tall = jnp.sum(jnp.where(square_r == square_c, row, 0.0), axis=1, keepdims=True)
+        lives.append(jnp.broadcast_to(tall, (every_blend, LANES)))
+
+    def split(u):
+        return u // cuts, pl.ds(u % cuts * some, some)
+
+    def local_sum(u):
+        q, h = u // cuts, u % cuts
+        if h == 0:
+            for copy in in_copy(q):
+                copy.wait()
 
         def one(c, carry):
             for p in range(ne):
@@ -99,7 +106,7 @@
                 stage[1, q, py * nx + px, c] = wsum
             return carry
 
-        lax.fori_loop(0, bands, one, 0)
+        lax.fori_loop(h * some, (h + 1) * some, one, 0)
 
     def line(a, first):
         along_x = (a == 0) == first
@@ -109,38 +116,41 @@
         along_x = (a == 0) == first
         return (y * nx + where if along_x else where * nx + x, j)
 
-    def s1(a, q, d):
+    def s1(a, u, d):
+        q, some_bands = split(u)
         at, n = line(a, True)
         other = line(a, False)[1]
         to = lax.rem(at + d, n)
         return pltpu.make_async_remote_copy(
-            src_ref=stage.at[a, q, pl.ds(to * other, other)],
-            dst_ref=land1.at[a, q, d - 1],
-            send_sem=s1_send.at[a, q, d - 1], recv_sem=s1_recv.at[a, q, d - 1],
+            src_ref=stage.at[a, q, pl.ds(to * other, other), some_bands],
+            dst_ref=land1.at[a, q, d - 1, pl.ds(0, other), some_bands],
+            send_sem=s1_send.at[a, u, d - 1], recv_sem=s1_recv.at[a, u, d - 1],
             device_id=device_at(a, True, to), device_id_type=MESH,
         )
 
-    def s2(a, q, d):
+    def s2(a, u, d):
+        q, some_bands = split(u)
         at, n = line(a, False)
         to = lax.rem(at + d, n)
         return pltpu.make_async_remote_copy(
-            src_ref=part.at[a, q, to],
-            dst_ref=land2.at[a, q, d - 1],
-            send_sem=s2_send.at[a, q, d - 1], recv_sem=s2_recv.at[a, q, d - 1],
+            src_ref=part.at[a, q, to, some_bands],
+            dst_ref=land2.at[a, q, d - 1, some_bands],
+            send_sem=s2_send.at[a, u, d - 1], recv_sem=s2_recv.at[a, u, d - 1],
             device_id=device_at(a, False, to), device_id_type=MESH,
         )
 
-    def s1_start(q):
+    def s1_start(u):
         for a in range(2):
             for d in range(1, line(a, True)[1]):
-                s1(a, q, d).start()
-
-    def s2_start(q):
+                s1(a, u, d).start()
+
+    def s2_start(u):
+        q, h = u // cuts, u % cuts
         for a in range(2):
             at, n = line(a, True)
             others = line(a, False)[1]
             for d in range(1, n):
-                s1(a, q, d).wait_recv()
+                s1(a, u, d).wait_recv()
 
             def add(c, carry):
                 for o in range(others):
@@ -150,55 +160,62 @@
                     part[a, q, o, c] = v
                 return carry
 
-            lax.fori_loop(0, bands, add, 0)
+            lax.fori_loop(h * some, (h + 1) * some, add, 0)
             for d in range(1, others):
-                s2(a, q, d).start()
-
-    here = home_e == e
-
-    def landing(q):
-        lanes = pl.ds(pl.multiple_of(e * LANES, LANES), LANES)
-        return pieces.at[q, :, :, home_slot, :, lanes]
-
-    def s3_local(q):
-        return pltpu.make_async_copy(final.at[q, j], landing(q), s3_recv.at[q])
-
-    def s3_remote(q, to):
+                s2(a, u, d).start()
+
+    def s3(u, d):
+        to = lax.rem(j + d, nb)
         return pltpu.make_async_remote_copy(
-            src_ref=final.at[q, to], dst_ref=landing(q),
-            send_sem=s3_send.at[q, to], recv_sem=s3_recv.at[q],
-            device_id=(home_e, to), device_id_type=MESH,
-        )
-
-    def s3_start(q):
+            src_ref=final.at[u, to], dst_ref=column.at[u, j],
+            send_sem=s3_send.at[u, d - 1], recv_sem=s3_recv.at[u, d - 1],
+            device_id=(e, to), device_id_type=MESH,
+        )
+
+    def s3_own(u):
+        return pltpu.make_async_copy(final.at[u, j], column.at[u, j], s3_send.at[u, nb - 1])
+
+    def s3_start(u):
+        q, h = u // cuts, u % cuts
         for a in range(2):
             at, n = line(a, False)
             for d in range(1, n):
-                s2(a, q, d).wait_recv()
-
-            def add(c, carry):
+                s2(a, u, d).wait_recv()
+
+            def add(i, carry):
+                c = h * some + i
                 v = part[a, q, at, c]
                 for d in range(1, n):
                     v = v + land2[a, q, d - 1, c]
                 for to in range(nb):
-                    final[q, to, a, c] = v[to * owned : (to + 1) * owned, :]
+                    final[u, to, a, i] = v[to * owned : (to + 1) * owned, :]
                 return carry
 
-            lax.fori_loop(0, bands, add, 0)
-
-        def send(d, carry):
-            s3_remote(q, lax.rem(j + d, nb)).start()
-            return carry
-
-        lax.fori_loop(1, nb, send, 0)
-
-        @pl.when(here)
-        def _():
-            s3_local(q).start()
-
-        @pl.when(jnp.logical_not(here))
-        def _():
-            s3_remote(q, j).start()
+            lax.fori_loop(0, some, add, 0)
+        s3_own(u).start()
+        for d in range(1, nb):
+            s3(u, d).start()
+
+    def s4(u, d):
+        to = lax.rem(e + d, ne)
+        return pltpu.make_async_remote_copy(
+            src_ref=column.at[u, pl.ds(to * per_dest, per_dest)], dst_ref=pieces.at[u, e],
+            send_sem=s4_send.at[u, d - 1], recv_sem=s4_recv.at[u, d - 1],
+            device_id=(to, j), device_id_type=MESH,
+        )
+
+    def s4_own(u):
+        return pltpu.make_async_copy(
+            column.at[u, pl.ds(e * per_dest, per_dest)], pieces.at[u, e], s4_send.at[u, ne - 1]
+        )
+
+    def s4_start(u):
+        s3_own(u).wait()
+        for d in range(1, nb):
+            s3(u, d).wait_recv()
+        for d in range(ne - 1, 0, -1):
+            s4(u, d).start()
+        s4_own(u).start()
 
     sub = lax.broadcasted_iota(jnp.int32, (held, LANES), 0)
     lane = lax.broadcasted_iota(jnp.int32, (held, LANES), 1)
@@ -271,21 +288,27 @@
             acc[k, bands] = v
 
     def finish(q):
-        pltpu.make_async_copy(pieces.at[q], pieces.at[q], s3_recv.at[q]).wait()
-        at = slice(q * width, (q + 1) * width)
-
-        def unpack(c, carry):
-            for s in range(per_dest):
-                rows = slice(s * owned, (s + 1) * owned)
-                wsum = pieces[q, 1, c, s]
-                inv = 1.0 / (1.0 + wsum)
-                flux = pieces[q, 0, c, s] * inv
-                coadd_ref[c, :, s * block + q * width : s * block + (q + 1) * width] = flux
-                flux_c[c, rows, at] = flux
-                cover[c, rows, at] = wsum * inv
-            return carry
-
-        lax.fori_loop(0, bands, unpack, 0)
+        for h in range(cuts):
+            u = q * cuts + h
+            s4_own(u).wait()
+            for d in range(1, ne):
+                s4(u, d).wait_recv()
+
+            def unpack(i, carry, u=u, h=h):
+                c = h * some + i
+                for p in range(ne):
+                    at = q * width + p * LANES
+                    for s in range(per_dest):
+                        rows = slice(s * owned, (s + 1) * owned)
+                        wsum = pieces[u, p, s, 1, i]
+                        inv = 1.0 / (1.0 + wsum)
+                        flux = pieces[u, p, s, 0, i] * inv
+                        coadd_ref[c, :, s * block + at : s * block + at + LANES] = flux
+                        flux_c[c, rows, at : at + LANES] = flux
+                        cover[c, rows, at : at + LANES] = wsum * inv
+                return carry
+
+            lax.fori_loop(0, some, unpack, 0)
 
         def go(i, carry):
             deblend(q * width + i * (group * LANES), True)
@@ -331,9 +354,9 @@
     local_sum(0)
     pl.semaphore_wait(barrier, total - 1)
     s1_start(0)
-    if chunks > 1:
-        local_sum(1)
-        s1_start(1)
+    for u in range(1, min(AHEAD, units)):
+        local_sum(u)
+        s1_start(u)
     for copy in side:
         copy.start()
 
@@ -344,19 +367,21 @@
             spectra[k, c] = jnp.concatenate([start] * per_dest, axis=0)
     steps()
 
-    for q in range(chunks + 2):
-        if q < chunks:
-            s2_start(q)
-        if q + 2 < chunks:
-            local_sum(q + 2)
-            s1_start(q + 2)
-        if 0 <= q - 1 < chunks:
-            s3_start(q - 1)
-        if q == 2:
+    for u in range(units + 3):
+        if u < units:
+            s2_start(u)
+        if u + AHEAD < units:
+            local_sum(u + AHEAD)
+            s1_start(u + AHEAD)
+        if 0 <= u - 1 < units:
+            s3_start(u - 1)
+        if 0 <= u - 2 < units:
+            s4_start(u - 2)
+        if u == 3:
             for copy in side:
                 copy.wait()
-        if 0 <= q - 2 < chunks:
-            finish(q - 2)
+        if 0 <= u - 3 < units and (u - 3) % cuts == cuts - 1:
+            finish((u - 3) // cuts)
 
     update(0)
     for it in range(1, ITERS):
@@ -375,23 +400,16 @@
             out = jnp.where(lane == k, spectra[k, c], out)
         spec_out[c] = out[0:owned, :slots]
 
-    for q in range(chunks):
+    for u in range(units):
         for a in range(2):
             for d in range(1, line(a, True)[1]):
-                s1(a, q, d).wait_send()
+                s1(a, u, d).wait_send()
             for d in range(1, line(a, False)[1]):
-                s2(a, q, d).wait_send()
-
-        def sent(d, carry, q=q):
-            s3_remote(q, lax.rem(j + d, nb)).wait_send()
-            return carry
-
-        lax.fori_loop(1, nb, sent, 0)
-
-        @pl.when(jnp.logical_not(here))
-        def _(q=q):
-            s3_remote(q, j).wait_send()
-
+                s2(a, u, d).wait_send()
+        for d in range(1, nb):
+            s3(u, d).wait_send()
+        for d in range(1, ne):
+            s4(u, d).wait_send()
     for it in range(ITERS):
         for d in range(1, ne):
             ps_copy(it, d).wait_send()
@@ -425,6 +443,8 @@
     held = per_dest * owned
     hop = max(nx, ny) - 1
     line = max(nx, ny)
+    cuts = 2 if bands % 2 == 0 else 1
+    units, some = chunks * cuts, bands // cuts
     f32 = jnp.float32
     vmem, smem, hbm = (pl.BlockSpec(memory_space=s) for s in (pltpu.VMEM, pltpu.SMEM, pl.ANY))
     dma = pltpu.SemaphoreType.DMA
@@ -447,25 +467,28 @@
             pltpu.VMEM((2, chunks, hop, line, bands, every_blend, LANES), f32),
             pltpu.VMEM((2, chunks, line, bands, every_blend, LANES), f32),
             pltpu.VMEM((2, chunks, hop, bands, every_blend, LANES), f32),
-            pltpu.VMEM((chunks, nb, 2, bands, owned, LANES), f32),
-            pltpu.VMEM((chunks, 2, bands, per_dest, owned, width), f32),
+            pltpu.VMEM((units, nb, 2, some, owned, LANES), f32),
+            pltpu.VMEM((units, nb, 2, some, owned, LANES), f32),
+            pltpu.VMEM((units, ne, per_dest, 2, some, owned, LANES), f32),
             pltpu.VMEM((slots, bands, held, LANES), f32),
             pltpu.VMEM((slots, held, LANES), f32),
             pltpu.VMEM((slots, bands + 1, held, LANES), f32),
             pltpu.VMEM((ITERS, ne, held, LANES), f32),
             dma((2, chunks)),
             dma((2, held)),
-            dma((2, chunks, hop)),
-            dma((2, chunks, hop)),
-            dma((2, chunks, hop)),
-            dma((2, chunks, hop)),
-            dma((chunks, nb)),
-            dma((chunks,)),
+            dma((2, units, hop)),
+            dma((2, units, hop)),
+            dma((2, units, hop)),
+            dma((2, units, hop)),
+            dma((units, nb)),
+            dma((units, nb - 1)),
+            dma((units, ne)),
+            dma((units, ne - 1)),
             dma((ITERS, ne - 1)),
             dma((ITERS, ne - 1)),
         ],
         compiler_params=pltpu.CompilerParams(
-            collective_id=0, has_side_effects=True, vmem_limit_bytes=62 * 2**20
+            collective_id=0, has_side_effects=True, vmem_limit_bytes=58 * 2**20
         ),
     )(visit_flux.transpose(0, 2, 1, 3), visit_precision.transpose(0, 2, 1, 3), visit_live,
       footprint, source_count, spectra_init.transpose(2, 0, 1), morphology_init)

time: 61.4 us -> 65.4 us (1.065)
  Pallas kernels: 57.7 us -> 61.7 us
    pallas_call x1, Pallas kernels: 56.7 us -> 60.7 us  [fused(): pl.pallas_call(functools.partial(coadd_kernel, ne=ne, nb=nb, ny=ny, nx=nx...]
where the time goes in v3:
time: 65.4 us; the launch traced here: 65.1 us
  Pallas kernels  61.7 us (94%)
  local copies, waits for them, and re-layouts  2.74 us (4%)
    pallas_call x1, Pallas kernels, fused(): pl.pallas_call(functools.partial(coadd_kernel, ne=ne, nb=nb, ny=ny, nx=nx...  60.7 us
    unnamed x6, local copies, waits for them, and re-layouts  2.74 us

profile of v3, /device:TPU:0, one launch (start us, length us, event | category | flops | bytes accessed | tf_op | source)
XLA Modules:
  0.0 65.1 jit_solution(10929891842000780389)
XLA Ops:
  0.6 60.7 %shard_map.94 = (f32[6,4,4096]{2,1,0:T(4,128)}, f32[6,4,8]{2,1,0:T(4,128)}, f32[8,8,2048]{2,1,0:T(8,128)}) custom-call(bf16[4,6,32,2048]{3,2,1,0:T(8,128)(2,1)} %bitcast.5, bf16[4,6,32,2048]{3,2,1,0:T(8,128)(2,1)} %bitcast.6, s32[4,32]{1,0:T(4,128)} %live_ref.1, s32[4,8,4096]{2,1,0:T(8,128)} %foot_hbm.1, s32[4]{0:T(128)} %count_ref.1, f32[6,4,8]{2,1,0:T(4,128)} %bitcast.7, ...), custom_call_target="tpu_custom_call" | custom-call | tf_op jit(solution)/shard_map/pallas_call | solution.py:451
  61.3 0.0 copy-start
  61.3 1.0 %copy-done = f32[8,8,2048]{2,1,0:T(8,128)S(1)} copy-done((f32[8,8,2048]{2,1,0:T(8,128)S(1)}, f32[8,8,2048]{2,1,0:T(8,128)}, u32[]{:S(2)}) %copy-start) | copy-done | bytes 524312
  62.4 0.0 copy-start.1
  62.4 1.0 %copy-done.1 = f32[6,4,4096]{2,1,0:T(4,128)S(1)} copy-done((f32[6,4,4096]{2,1,0:T(4,128)S(1)}, f32[6,4,4096]{2,1,0:T(4,128)}, u32[]{:S(2)}) %copy-start.1) | copy-done | bytes 393240
  63.4 0.0 copy-start.2
  63.4 0.7 %copy-done.2 = f32[6,4,8]{2,1,0:T(4,128)S(1)} copy-done((f32[6,4,8]{2,1,0:T(4,128)S(1)}, f32[6,4,8]{2,1,0:T(4,128)}, u32[]{:S(2)}) %copy-start.2) | copy-done | bytes 792
  64.1 1.0 %shard_map.95 = (f32[6,4,4096]{2,1,0:T(4,128)}, f32[6,4,8]{2,1,0:T(4,128)}, f32[4,8,4096]{2,1,0:T(8,128)}) custom-call(f32[6,4,4096]{2,1,0:T(4,128)S(1)} %copy-done.1, f32[6,4,8]{2,1,0:T(4,128)S(1)} %copy-done.2, f32[8,8,2048]{2,1,0:T(8,128)S(1)} %copy-done), custom_call_target="tpu_custom_call" | custom-call | tf_op jit(solution)/shard_map/pallas_call | solution.py:495
Async XLA Ops:
  61.3 1.0 %copy-start = (f32[8,8,2048]{2,1,0:T(8,128)S(1)}, f32[8,8,2048]{2,1,0:T(8,128)}, u32[]{:S(2)}) copy-start(f32[8,8,2048]{2,1,0:T(8,128)} %get-tuple-element.11.morph_in) | copy-start | bytes 1572868
  62.4 1.0 %copy-start.1 = (f32[6,4,4096]{2,1,0:T(4,128)S(1)}, f32[6,4,4096]{2,1,0:T(4,128)}, u32[]{:S(2)}) copy-start(f32[6,4,4096]{2,1,0:T(4,128)} %get-tuple-element.9.coadd_in) | copy-start | bytes 1179652
  63.4 0.7 %copy-start.2 = (f32[6,4,8]{2,1,0:T(4,128)S(1)}, f32[6,4,8]{2,1,0:T(4,128)}, u32[]{:S(2)}) copy-start(f32[6,4,8]{2,1,0:T(4,128)} %get-tuple-element.10.spec_in) | copy-start | bytes 2308

commit v4 on v2

--- a/solution.py
+++ b/solution.py
@@ -431,9 +431,9 @@
     parts = pl.pallas_call(
         functools.partial(coadd_kernel, ne=ne, nb=nb, ny=ny, nx=nx),
         out_shape=(
-            jax.ShapeDtypeStruct((bands, owned, pix_part), f32),
-            jax.ShapeDtypeStruct((bands, owned, slots), f32),
-            jax.ShapeDtypeStruct((slots, held, block), f32),
+            pltpu.VMEM((bands, owned, pix_part), f32),
+            pltpu.VMEM((bands, owned, slots), f32),
+            pltpu.VMEM((slots, held, block), f32),
         ),
         in_specs=[hbm, hbm, vmem, hbm, smem, vmem, hbm],
         out_specs=(vmem, vmem, vmem),
@@ -465,7 +465,7 @@
             dma((ITERS, ne - 1)),
         ],
         compiler_params=pltpu.CompilerParams(
-            collective_id=0, has_side_effects=True, vmem_limit_bytes=62 * 2**20
+            collective_id=0, has_side_effects=True, vmem_limit_bytes=58 * 2**20
         ),
     )(visit_flux.transpose(0, 2, 1, 3), visit_precision.transpose(0, 2, 1, 3), visit_live,
       footprint, source_count, spectra_init.transpose(2, 0, 1), morphology_init)

time: 61.4 us -> 57.6 us (0.938)
  local copies, waits for them, and re-layouts: 2.74 us -> 0 us
  Pallas kernels: 57.7 us -> 56.7 us
    unnamed x6 -> x0, local copies, waits for them, and re-layouts: 2.74 us -> none
    pallas_call x1, Pallas kernels: 56.7 us -> 55.7 us  [fused(): pl.pallas_call(functools.partial(coadd_kernel, ne=ne, nb=nb, ny=ny, nx=nx...]
where the time goes in v4:
time: 57.6 us; the launch traced here: 57.4 us
  Pallas kernels  56.7 us (98%)
  between operations  0.64 us (1%)
    pallas_call x1, Pallas kernels, fused(): pl.pallas_call(functools.partial(coadd_kernel, ne=ne, nb=nb, ny=ny, nx=nx...  55.7 us

profile of v4, /device:TPU:0, one launch (start us, length us, event | category | flops | bytes accessed | tf_op | source)
XLA Modules:
  0.0 57.4 jit_solution(11928125684936701673)
XLA Ops:
  0.6 55.7 %shard_map.94 = (f32[6,4,4096]{2,1,0:T(4,128)S(1)}, f32[6,4,8]{2,1,0:T(4,128)S(1)}, f32[8,8,2048]{2,1,0:T(8,128)S(1)}) custom-call(bf16[4,6,32,2048]{3,2,1,0:T(8,128)(2,1)} %bitcast.5, bf16[4,6,32,2048]{3,2,1,0:T(8,128)(2,1)} %bitcast.6, s32[4,32]{1,0:T(4,128)} %live_ref.1, s32[4,8,4096]{2,1,0:T(8,128)} %foot_hbm.1, s32[4]{0:T(128)} %count_ref.1, ...), custom_call_target="tpu_custom_call" | custom-call | tf_op jit(solution)/shard_map/pallas_call | solution.py:431
  56.4 1.0 %shard_map.95 = (f32[6,4,4096]{2,1,0:T(4,128)}, f32[6,4,8]{2,1,0:T(4,128)}, f32[4,8,4096]{2,1,0:T(8,128)}) custom-call(f32[6,4,4096]{2,1,0:T(4,128)S(1)} %get-tuple-element.9.coadd_in, f32[6,4,8]{2,1,0:T(4,128)S(1)} %get-tuple-element.10.spec_in, f32[8,8,2048]{2,1,0:T(8,128)S(1)} %get-tuple-element.11.morph_in), custom_call_target="tpu_custom_call" | custom-call | tf_op jit(solution)/shard_map/pallas_call | solution.py:472
